TPU v7x, 32 devices: a whole 2x2x4 slice. The times are simulated.
32 devices in a mesh: bx: 8 (over y, x, core), by: 4 (over z).
Axes of the slice: x: 2, y: 2, z: 4, core: 2. Of those that a mesh axis runs over, the one named last changes fastest.
Arguments:
- photon_data: float32 [6, 512, 128, 128], P(None, 'bx', 'by'), may hold values from 0 to 1, as said below
- block_counts: int32 [512, 128], P('bx', 'by'), may hold values from 1 to 128
- gather_offsets: float32 [3, 131072], P(None, ('bx', 'by')), may hold values from 0 to 1, as said below
- gather_blocks: int32 [4, 131072], P(None, ('bx', 'by')), may hold values from 0 to 65535, as said below
- albedo: float32 [3, 131072], P(None, ('bx', 'by')), may hold values from 0.1 to 1
- gather_pixels: int32 [131072], P(('bx', 'by')), may hold values from 0 to 65535, as said below
- tile_slot: int32 [256], replicated, may hold values from 0 to 255, as said below
Outputs:
- film: float32 [3, 256, 256], P(None, ('bx', 'by'))
Inputs may be any that keep to these rules, and one draw needn't show every extreme that they name: `photon_data`: per point and channel in cell units: entries 0 to 2 are a position in [0, 1), entries 3 to 5 a positive power. `gather_offsets`: each coordinate lies in [0, 1). `gather_blocks`: entry 0 is the point's own cell, inside the brick of the device that holds the point; the 4 entries are the four different cells of a 2 x 2 square of cells (periodic) that contains it. `gather_pixels`: in the rows of one device, at most 384 gather points lie in tiles whose slots s share s // 8; in every draw some such owner group receives exactly 384 from every device. `tile_slot`: A permutation of 0 to 255.
All inputs are finite; a program needn't handle non-finite values.
Results may differ from a plain program's by a relative error of at most 0.0003.
Values sent between devices are 32-bit elements; how exact they have to be, the bound alone decides.
A program may use at most 512 MiB of HBM per device.

v0:
```python
import jax
import jax.numpy as jnp
from jax import lax
from jax.sharding import PartitionSpec as P

TILE_PIX = 256


RADIUS_SQ = 0.25


def extended(x, sides, width):
    for axis, dim in sides:
        peers, length = (lax.axis_size(axis), x.shape[dim])
        up = [(i, (i + 1) % peers) for i in range(peers)]
        down = [(j, i) for i, j in up]
        last = lax.slice_in_dim(x, length - width, length, axis=dim)
        initial = lax.slice_in_dim(x, 0, width, axis=dim)
        before = lax.ppermute(last, axis, up)
        after = lax.ppermute(initial, axis, down)
        x = jnp.concatenate([before, x, after], axis=dim)
    return x


def kernel_sum(blocks, shift_x, shift_y, offsets, albedo):
    delta_x = shift_x[:, :, None] + blocks[0] - offsets[0][:, None, None]
    delta_y = shift_y[:, :, None] + blocks[1] - offsets[1][:, None, None]
    delta_z = blocks[2] - offsets[2][:, None, None]
    dist_sq = delta_x * delta_x + delta_y * delta_y + delta_z * delta_z
    weight = jnp.maximum(1.0 - dist_sq / RADIUS_SQ, 0.0)
    sums = jnp.sum(weight[None] * blocks[3:6], axis=(2, 3))
    return albedo * sums


def per_device(
    photon_data, block_counts, gather_offsets, gather_blocks, albedo, gather_pixels, tile_slot
):
    cells_x, cells_y, slots = (photon_data.shape[1], photon_data.shape[2], photon_data.shape[3])
    span_x = lax.axis_size("bx")
    span_y = lax.axis_size("by")
    grid_x = cells_x * span_x
    grid_y = cells_y * span_y
    occupied = (
        lax.broadcasted_iota(jnp.int32, (cells_x, cells_y, slots), 2) < block_counts[:, :, None]
    )
    photons = jnp.concatenate(
        [photon_data[:3], photon_data[3:] * occupied.astype(jnp.float32)[None]], axis=0
    )
    padded = extended(photons, (("bx", 1), ("by", 2)), 1)
    table = padded.reshape(6, (cells_x + 2) * (cells_y + 2), slots)
    first_x = lax.axis_index("bx") * cells_x
    first_y = lax.axis_index("by") * cells_y
    local_x = (gather_blocks // grid_y - first_x + 1) % grid_x
    local_y = (gather_blocks % grid_y - first_y + 1) % grid_y
    shift_x = (local_x - local_x[:1]).astype(jnp.float32)
    shift_y = (local_y - local_y[:1]).astype(jnp.float32)
    index = local_x * (cells_y + 2) + local_y
    listed = gather_blocks.shape[0]
    points = gather_offsets.shape[1]
    group = min(512, points)
    groups = points // group
    idx_stack = index.reshape(listed, groups, group).transpose(1, 2, 0)
    sx_stack = shift_x.reshape(listed, groups, group).transpose(1, 2, 0)
    sy_stack = shift_y.reshape(listed, groups, group).transpose(1, 2, 0)
    off_stack = gather_offsets.reshape(3, groups, group).transpose(1, 0, 2)
    alb_stack = albedo.reshape(3, groups, group).transpose(1, 0, 2)

    def one_group(packed):
        idb, move_x, move_y, off, alb = packed
        blocks = jnp.take(table, idb.reshape(-1), axis=1).reshape(6, group, listed, slots)
        return kernel_sum(blocks, move_x, move_y, off, alb)

    rad = lax.map(one_group, (idx_stack, sx_stack, sy_stack, off_stack, alb_stack))
    radiance = rad.transpose(1, 0, 2).reshape(3, points)
    tiles = tile_slot.shape[0]
    tile = gather_pixels // TILE_PIX
    matched = tile[:, None] == jnp.arange(tiles, dtype=jnp.int32)[None, :]
    slot = jnp.sum(jnp.where(matched, tile_slot[None, :], 0), axis=1)
    within_tile = gather_pixels % TILE_PIX
    target = slot * TILE_PIX + within_tile
    partial_film = jnp.zeros((3, tiles * TILE_PIX), jnp.float32).at[:, target].add(radiance)
    partial_film = partial_film.reshape(3, tiles, TILE_PIX)
    return lax.psum_scatter(partial_film, ("bx", "by"), scatter_dimension=1, tiled=True)


def solution(mesh):
    in_specs = (
        P(None, "bx", "by", None),
        P("bx", "by"),
        P(None, ("bx", "by")),
        P(None, ("bx", "by")),
        P(None, ("bx", "by")),
        P(("bx", "by")),
        P(),
    )
    out_specs = P(None, ("bx", "by"), None)
    return jax.shard_map(
        per_device, mesh=mesh, in_specs=in_specs, out_specs=out_specs, check_vma=False
    )
```

profile of v0, /device:TPU:0, one launch (start us, length us, event | category | flops | bytes accessed | tf_op | source)
XLA Modules:
  0.0 604.1 jit_solution(11411752718911548168)
XLA Ops:
  7.7 3.7 fusion.16
  11.5 1.6 copy-done
  14.2 2.9 collective-permute-start.1
  18.1 2.6 select_reduce_fusion
  20.6 2.0 copy.55
  22.7 2.0 copy.49
  24.7 2.0 copy.48
  26.7 1.8 pad_maximum_fusion.4
  28.6 4.4 collective-permute-start.3
  33.0 5.8 collective-permute-done.3
  39.0 3.4 collective-permute-done.2
  42.7 3.1 pad_maximum_fusion
  45.8 5.8 copy.60
  51.6 354.3 %while.10 = (s32[]{:T(128)}, f32[8,3,512]{2,1,0:T(4,128)S(1)}, f32[8,3,512]{2,1,0:T(4,128)}, f32[8,512,4]{2,1,0:T(8,128)}, s32[8,512,4]{2,1,0:T(8,128)}, /*index...) while((s32[]{:T(128)}, f32[8,3,512]{2,1,0:T(4,128)S(1)}, ...), condition=%wide.region_4.5_spmd, body=%wide.region_1.4_spmd.sunk | while | flops 6574084 | bytes 40237240 | solution.py:73
  54.7 1.1 constant_dynamic-slice_fusion.11
  56.1 19.4 %gather_fusion = f32[2048,6,128]{2,1,0:T(8,128)} fusion(f32[6,2244,128]{2,0,1:T(8,128)} %get-tuple-element.211, s32[2048]{0:T(1024)S(1)} %broadcast_clamp_fusion.2), kind=kCustom, calls=%fused_computation.clone.1 | custom fusion | bytes 12591104 | tf_op jit(solution)/shard_map/while/body/eval_jaxpr/jit(_take)/gather | solution.py:70
  75.4 11.2 %select_bitcast_fusion.2 = f32[6,2048,128]{2,0,1:T(8,128)S(1)} fusion(f32[2048,6,128]{2,1,0:T(8,128)} %gather_fusion, pred[2048]{0:T(1024)(128)(4,1)S(1)} %compare_and_fusion.2), kind=kLoop, calls=%fused_computation.2.clone.1 | loop fusion | flops 1572864 | bytes 12584960 | tf_op jit(solution)/shard_map/while/body/eval_jaxpr/jit(_take)/select_n | solution.py:70
  86.6 2.2 fusion.20
  88.9 1.9 subtract_maximum_fusion.2
  90.7 3.6 fusion.21
  98.9 1.1 constant_dynamic-slice_fusion.11
  100.3 19.4 %gather_fusion = f32[2048,6,128]{2,1,0:T(8,128)} fusion(f32[6,2244,128]{2,0,1:T(8,128)} %get-tuple-element.211, s32[2048]{0:T(1024)S(1)} %broadcast_clamp_fusion.2), kind=kCustom, calls=%fused_computation.clone.1 | custom fusion | bytes 12591104 | tf_op jit(solution)/shard_map/while/body/eval_jaxpr/jit(_take)/gather | solution.py:70
  119.7 11.2 %select_bitcast_fusion.2 = f32[6,2048,128]{2,0,1:T(8,128)S(1)} fusion(f32[2048,6,128]{2,1,0:T(8,128)} %gather_fusion, pred[2048]{0:T(1024)(128)(4,1)S(1)} %compare_and_fusion.2), kind=kLoop, calls=%fused_computation.2.clone.1 | loop fusion | flops 1572864 | bytes 12584960 | tf_op jit(solution)/shard_map/while/body/eval_jaxpr/jit(_take)/select_n | solution.py:70
  130.9 2.2 fusion.20
  133.1 1.9 subtract_maximum_fusion.2
  135.0 3.6 fusion.21
  143.2 1.1 constant_dynamic-slice_fusion.11
  144.6 19.4 %gather_fusion = f32[2048,6,128]{2,1,0:T(8,128)} fusion(f32[6,2244,128]{2,0,1:T(8,128)} %get-tuple-element.211, s32[2048]{0:T(1024)S(1)} %broadcast_clamp_fusion.2), kind=kCustom, calls=%fused_computation.clone.1 | custom fusion | bytes 12591104 | tf_op jit(solution)/shard_map/while/body/eval_jaxpr/jit(_take)/gather | solution.py:70
  164.0 11.2 %select_bitcast_fusion.2 = f32[6,2048,128]{2,0,1:T(8,128)S(1)} fusion(f32[2048,6,128]{2,1,0:T(8,128)} %gather_fusion, pred[2048]{0:T(1024)(128)(4,1)S(1)} %compare_and_fusion.2), kind=kLoop, calls=%fused_computation.2.clone.1 | loop fusion | flops 1572864 | bytes 12584960 | tf_op jit(solution)/shard_map/while/body/eval_jaxpr/jit(_take)/select_n | solution.py:70
  175.2 2.2 fusion.20
  177.4 1.9 subtract_maximum_fusion.2
  179.3 3.6 fusion.21
  187.5 1.1 constant_dynamic-slice_fusion.11
  188.9 19.4 %gather_fusion = f32[2048,6,128]{2,1,0:T(8,128)} fusion(f32[6,2244,128]{2,0,1:T(8,128)} %get-tuple-element.211, s32[2048]{0:T(1024)S(1)} %broadcast_clamp_fusion.2), kind=kCustom, calls=%fused_computation.clone.1 | custom fusion | bytes 12591104 | tf_op jit(solution)/shard_map/while/body/eval_jaxpr/jit(_take)/gather | solution.py:70
  208.3 11.2 %select_bitcast_fusion.2 = f32[6,2048,128]{2,0,1:T(8,128)S(1)} fusion(f32[2048,6,128]{2,1,0:T(8,128)} %gather_fusion, pred[2048]{0:T(1024)(128)(4,1)S(1)} %compare_and_fusion.2), kind=kLoop, calls=%fused_computation.2.clone.1 | loop fusion | flops 1572864 | bytes 12584960 | tf_op jit(solution)/shard_map/while/body/eval_jaxpr/jit(_take)/select_n | solution.py:70
  219.5 2.2 fusion.20
  221.7 1.9 subtract_maximum_fusion.2
  223.6 3.6 fusion.21
  231.8 1.1 constant_dynamic-slice_fusion.11
  233.2 19.4 %gather_fusion = f32[2048,6,128]{2,1,0:T(8,128)} fusion(f32[6,2244,128]{2,0,1:T(8,128)} %get-tuple-element.211, s32[2048]{0:T(1024)S(1)} %broadcast_clamp_fusion.2), kind=kCustom, calls=%fused_computation.clone.1 | custom fusion | bytes 12591104 | tf_op jit(solution)/shard_map/while/body/eval_jaxpr/jit(_take)/gather | solution.py:70
  252.6 11.2 %select_bitcast_fusion.2 = f32[6,2048,128]{2,0,1:T(8,128)S(1)} fusion(f32[2048,6,128]{2,1,0:T(8,128)} %gather_fusion, pred[2048]{0:T(1024)(128)(4,1)S(1)} %compare_and_fusion.2), kind=kLoop, calls=%fused_computation.2.clone.1 | loop fusion | flops 1572864 | bytes 12584960 | tf_op jit(solution)/shard_map/while/body/eval_jaxpr/jit(_take)/select_n | solution.py:70
  263.8 2.2 fusion.20
  266.0 1.9 subtract_maximum_fusion.2
  267.9 3.6 fusion.21
  276.1 1.1 constant_dynamic-slice_fusion.11
  277.5 19.4 %gather_fusion = f32[2048,6,128]{2,1,0:T(8,128)} fusion(f32[6,2244,128]{2,0,1:T(8,128)} %get-tuple-element.211, s32[2048]{0:T(1024)S(1)} %broadcast_clamp_fusion.2), kind=kCustom, calls=%fused_computation.clone.1 | custom fusion | bytes 12591104 | tf_op jit(solution)/shard_map/while/body/eval_jaxpr/jit(_take)/gather | solution.py:70
  296.9 11.2 %select_bitcast_fusion.2 = f32[6,2048,128]{2,0,1:T(8,128)S(1)} fusion(f32[2048,6,128]{2,1,0:T(8,128)} %gather_fusion, pred[2048]{0:T(1024)(128)(4,1)S(1)} %compare_and_fusion.2), kind=kLoop, calls=%fused_computation.2.clone.1 | loop fusion | flops 1572864 | bytes 12584960 | tf_op jit(solution)/shard_map/while/body/eval_jaxpr/jit(_take)/select_n | solution.py:70
  308.1 2.2 fusion.20
  310.3 1.9 subtract_maximum_fusion.2
  312.2 3.6 fusion.21
  320.4 1.1 constant_dynamic-slice_fusion.11
  321.8 19.4 %gather_fusion = f32[2048,6,128]{2,1,0:T(8,128)} fusion(f32[6,2244,128]{2,0,1:T(8,128)} %get-tuple-element.211, s32[2048]{0:T(1024)S(1)} %broadcast_clamp_fusion.2), kind=kCustom, calls=%fused_computation.clone.1 | custom fusion | bytes 12591104 | tf_op jit(solution)/shard_map/while/body/eval_jaxpr/jit(_take)/gather | solution.py:70
  341.1 11.2 %select_bitcast_fusion.2 = f32[6,2048,128]{2,0,1:T(8,128)S(1)} fusion(f32[2048,6,128]{2,1,0:T(8,128)} %gather_fusion, pred[2048]{0:T(1024)(128)(4,1)S(1)} %compare_and_fusion.2), kind=kLoop, calls=%fused_computation.2.clone.1 | loop fusion | flops 1572864 | bytes 12584960 | tf_op jit(solution)/shard_map/while/body/eval_jaxpr/jit(_take)/select_n | solution.py:70
  352.3 2.2 fusion.20
  354.6 1.9 subtract_maximum_fusion.2
  356.4 3.6 fusion.21
  366.0 19.4 %gather_fusion = f32[2048,6,128]{2,1,0:T(8,128)} fusion(f32[6,2244,128]{2,0,1:T(8,128)} %get-tuple-element.211, s32[2048]{0:T(1024)S(1)} %broadcast_clamp_fusion.2), kind=kCustom, calls=%fused_computation.clone.1 | custom fusion | bytes 12591104 | tf_op jit(solution)/shard_map/while/body/eval_jaxpr/jit(_take)/gather | solution.py:70
  385.4 11.2 %select_bitcast_fusion.2 = f32[6,2048,128]{2,0,1:T(8,128)S(1)} fusion(f32[2048,6,128]{2,1,0:T(8,128)} %gather_fusion, pred[2048]{0:T(1024)(128)(4,1)S(1)} %compare_and_fusion.2), kind=kLoop, calls=%fused_computation.2.clone.1 | loop fusion | flops 1572864 | bytes 12584960 | tf_op jit(solution)/shard_map/while/body/eval_jaxpr/jit(_take)/select_n | solution.py:70
  396.6 2.2 fusion.20
  398.8 1.9 subtract_maximum_fusion.2
  400.7 3.6 fusion.21
  406.5 35.5 %scatter_custom_fusion = f32[3,65536]{0,1:T(8,128)} fusion(s32[4096]{0:T(1024)S(1)} %compare_select_fusion.2, f32[4096,3]{1,0:T(8,128)S(1)} %copy.57, f32[]{:T(128)} %constant.112.clone.1), kind=kCustom, calls=%fused_computation.18 | custom fusion | flops 12288 | bytes 786436 | tf_op jit(solution)/shard_map/scatter-add | solution.py:81
  442.0 19.5 %copy.58 = f32[3,256,256]{2,1,0:T(8,128)} copy(f32[3,256,256]{0,2,1:T(8,128)} %bitcast.63) | data formatting | bytes 1572864 | tf_op jit(solution)/shard_map/reshape | solution.py:82
  461.6 135.7 %reduce-scatter.2.cloned.1.call-done = f32[3,8,256]{2,1,0:T(8,128)} async-done(((f32[3,256,256]{2,1,0:T(8,128)}), f32[3,8,256]{2,1,0:T(8,128)}) %reduce-scatter.2.cloned.1.call-update) | async-done | bytes 24592 | tf_op jit(solution)/shard_map/reduce_scatter | solution.py:83
  (177 shorter events, 44.0 us)
Async XLA Ops:
  6.5 590.7 %reduce-scatter.2.cloned.1.call-start = ((), (), s32[]{:S(2)}) async-start(), calls=%async_computation.1 | async-start | bytes 811008 | tf_op jit(solution)/shard_map/reduce_scatter | solution.py:83
  11.4 1.6 copy-start
  11.4 5.7 copy-start.3
  11.4 6.3 %copy-start.5 = (s32[4,4096]{1,0:T(4,128)S(1)}, s32[4,4096]{1,0:T(4,128)}, u32[]{:S(2)}) copy-start(s32[4,4096]{1,0:T(4,128)} %param.12) | copy-start | bytes 196612
  13.7 12.9 %collective-permute-start = (f32[6,1,32,128]{3,2,1,0:T(8,128)}, f32[6,1,32,128]{3,2,1,0:T(8,128)S(1)}, u32[]{:S(2)}, u32[]{:S(2)}) collective-permute-start(f32[6,1,32,128]{3,2,1,0:T(8,128)} %get-tuple-element.109), channel_id=1, source_target_pairs={{0,4},{4,8},{8,12},{12,16},{16,20},{20,24},{24,28},{28,0},{1,5},{5... | collective-permute-start | bytes 294920 | tf_op jit(solution)/shard_map/ppermute | solution.py:19
  14.2 12.4 %collective-permute-start.1 = (f32[6,1,32,128]{3,2,1,0:T(8,128)}, f32[6,1,32,128]{3,2,1,0:T(8,128)S(1)}, u32[]{:S(2)}, u32[]{:S(2)}) collective-permute-start(f32[6,1,32,128]{3,2,1,0:T(8,128)} %get-tuple-element.110), channel_id=1, source_target_pairs={{4,0},{8,4},{12,8},{16,12},{20,16},{24,20},{28,24},{0,28},{5,1},{9... | collective-permute-start | bytes 294920 | tf_op jit(solution)/shard_map/ppermute | solution.py:20
  22.7 10.3 %copy-start.4 = (s32[4096]{0:T(1024)S(1)}, s32[4096]{0:T(1024)}, u32[]{:S(2)}) copy-start(s32[4096]{0:T(1024)} %select_reduce_fusion) | copy-start | bytes 49156
  26.7 16.0 %copy-start.1 = (f32[3,64,32,128]{3,2,1,0:T(8,128)S(1)}, f32[3,64,32,128]{3,2,1,0:T(8,128)}, u32[]{:S(2)}) copy-start(f32[3,64,32,128]{3,2,1,0:T(8,128)} %copy-done) | copy-start | bytes 9437188
  28.6 10.2 %collective-permute-start.3 = (f32[6,66,1,128]{3,1,2,0:T(8,128)S(1)}, f32[6,66,1,128]{3,1,2,0:T(8,128)S(1)}, u32[]{:S(2)}, u32[]{:S(2)}) collective-permute-start(f32[6,66,1,128]{3,1,2,0:T(8,128)S(1)} %copy.52), channel_id=1, source_target_pairs={{1,0},{2,1},{3,2},{0,3},{5,4},{6,5},{7,6},{4,7},{9,8},{10,9},{11,1... | collective-permute-start | bytes 608264 | tf_op jit(solution)/shard_map/ppermute | solution.py:20
  33.0 9.5 %collective-permute-start.2 = (f32[6,66,1,128]{3,1,2,0:T(8,128)S(1)}, f32[6,66,1,128]{3,1,2,0:T(8,128)S(1)}, u32[]{:S(2)}, u32[]{:S(2)}) collective-permute-start(f32[6,66,1,128]{3,1,2,0:T(8,128)S(1)} %copy.51), channel_id=1, source_target_pairs={{0,1},{1,2},{2,3},{3,0},{4,5},{5,6},{6,7},{7,4},{8,9},{9,10},{10,1... | collective-permute-start | bytes 608264 | tf_op jit(solution)/shard_map/ppermute | solution.py:19
  45.8 5.8 copy-start.2
Sparse Core Ops, SparseCore 0:
  461.7 135.4 reduce-scatter.1
where the time goes:
time: 608 us; the launch traced here: 604 us
  local copies, waits for them, and re-layouts  243 us (40%)
  other arithmetic  194 us (32%)
  waiting for transfers between devices  145 us (24%)
  between operations  13.5 us (2%)
  starting transfers between devices  7.78 us (1%)
    gather x8, local copies, waits for them, and re-layouts, one_group(): jnp.take(table, idb.reshape(-1), axis=1).reshape(6, group, listed, slots)  155 us
    reduce_scatter x1, waiting for transfers between devices, per_device(): lax.psum_scatter(partial_film, ('bx', 'by'), scatter_dimension=1, tiled=T...  136 us
    select_n x16, other arithmetic, one_group(): jnp.take(table, idb.reshape(-1), axis=1).reshape(6, group, listed, slots)  89.7 us
    scatter-add x1, other arithmetic, per_device(): jnp.zeros((3, tiles * TILE_PIX), jnp.float32).at[:, target].add(radiance)  35.5 us
    reduce_sum x16, other arithmetic, kernel_sum(): sums = jnp.sum(weight[None] * blocks[3:6], axis=(2, 3))  34.3 us
    slice x16, local copies, waits for them, and re-layouts, kernel_sum(): delta_x = shift_x[:, :, None] + blocks[0] - offsets[0][:, None, None]  24.2 us
    reshape x1, local copies, waits for them, and re-layouts, per_device(): partial_film = partial_film.reshape(3, tiles, TILE_PIX)  19.5 us
    dynamic_slice x16, local copies, waits for them, and re-layouts, per_device(): lax.map(one_group, (idx_stack, sx_stack, sy_stack, off_stack, alb_stack))  16.4 us
  transfers between devices with their start and end apart: 5, of which 3 were waited for; matrix products, arithmetic and copies ran while one was open for 2% of the time, Pallas kernels for 0%

commit v1 on v0

v1 whole, which is shorter than its diff:
```python
import functools

import jax
import jax.numpy as jnp
from jax import lax
from jax.experimental import pallas as pl
from jax.experimental.pallas import tpu as pltpu
from jax.sharding import PartitionSpec as P

TILE_PIX = 256
INV_RADIUS_SQ = 4.0
FAR = 1.0e4
LANES = 128
MESH = pl.DeviceIdType.MESH
HIGHEST = lax.Precision.HIGHEST
NT = (((1,), (1,)), ((), ()))
GROUP = 32


def halo_kernel(nx, ny, cx, cy, send, recv, send_sem, recv_sem):
    ix, iy = lax.axis_index("bx"), lax.axis_index("by")
    right, left = lax.rem(ix + 1, nx), lax.rem(ix + nx - 1, nx)
    up, down = lax.rem(iy + 1, ny), lax.rem(iy + ny - 1, ny)
    peers = [
        (right, iy, 0, cy),
        (left, iy, cy, cy),
        (ix, up, 2 * cy, cx),
        (ix, down, 2 * cy + cx, cx),
        (right, up, 2 * cy + 2 * cx, 8),
        (right, down, 2 * cy + 2 * cx + 8, 8),
        (left, up, 2 * cy + 2 * cx + 16, 8),
        (left, down, 2 * cy + 2 * cx + 24, 8),
    ]
    barrier = pltpu.get_barrier_semaphore()
    for px, py, _, _ in peers:
        pl.semaphore_signal(barrier, inc=1, device_id=(px, py), device_id_type=MESH)
    pl.semaphore_wait(barrier, len(peers))
    copies = []
    for n, (px, py, first, rows) in enumerate(peers):
        part = pl.ds(first, rows)
        copies.append(
            pltpu.make_async_remote_copy(
                src_ref=send.at[:, part],
                dst_ref=recv.at[:, part],
                send_sem=send_sem.at[n],
                recv_sem=recv_sem.at[n],
                device_id=(px, py),
                device_id_type=MESH,
            )
        )
    for n in (2, 3, 0, 1, 4, 5, 6, 7):
        copies[n].start()
    for copy in copies:
        copy.wait()


def exchange_halo(send, nx, ny, cx, cy):
    return pl.pallas_call(
        functools.partial(halo_kernel, nx, ny, cx, cy),
        out_shape=jax.ShapeDtypeStruct(send.shape, jnp.float32),
        in_specs=[pl.BlockSpec(memory_space=pl.ANY)],
        out_specs=pl.BlockSpec(memory_space=pl.ANY),
        scratch_shapes=[pltpu.SemaphoreType.DMA((8,)), pltpu.SemaphoreType.DMA((8,))],
        compiler_params=pltpu.CompilerParams(collective_id=0, has_side_effects=True),
        name="halo",
    )(send)


def radiance_kernel(
    cells, rows, owners, cap_rows,
    idx, pts, alb, meta, first, rest, halo, out,
    table, stage, cols, acc, packed, tri, sems,
):
    listed = 4
    points = pts.shape[1]
    fills = [
        pltpu.make_async_copy(first, table.at[pl.ds(0, cells)], sems.at[0]),
    ]
    for c in range(1, 6):
        fills.append(
            pltpu.make_async_copy(rest.at[c], table.at[pl.ds(c * rows, cells)], sems.at[c])
        )
    for c in range(6):
        fills.append(
            pltpu.make_async_copy(
                halo.at[c], table.at[pl.ds(c * rows + cells, rows - cells)], sems.at[6 + c]
            )
        )
    for fill in fills:
        fill.start()
    a = lax.broadcasted_iota(jnp.int32, (LANES, LANES), 0)
    b = lax.broadcasted_iota(jnp.int32, (LANES, LANES), 1)
    tri[...] = jnp.where(a < b, 1.0, 0.0).astype(jnp.bfloat16)
    packed[...] = jnp.zeros_like(packed)
    for fill in fills:
        fill.wait()
    ones = jnp.ones((8, LANES), jnp.float32)
    own_iota = lax.broadcasted_iota(jnp.int32, (owners, LANES), 0)
    cap_iota = lax.broadcasted_iota(jnp.int32, (cap_rows * LANES, LANES), 0).astype(jnp.float32)

    def block(blk, carry):
        base = pl.multiple_of(blk * LANES, LANES)
        span = pl.ds(base, LANES)
        cols[...] = pts[:, span].T

        def some(sub, _):
            start = sub * GROUP
            for p in range(GROUP):
                for k in range(listed):
                    row = idx[k * points + base + start + p]
                    stage[pl.ds(k * 6 * GROUP + p, 6, stride=GROUP), :] = table[
                        pl.ds(row, 6, stride=rows), :
                    ]
            for q in range(GROUP // 8):
                place = pl.ds(pl.multiple_of(start + q * 8, 8), 8)
                col = cols[place, :]
                oz = jnp.broadcast_to(col[:, 8:9], (8, LANES))
                totals = [None] * 3
                for k in range(listed):
                    def chan(c):
                        return stage[pl.ds((k * 6 + c) * GROUP + q * 8, 8), :]
                    dx = chan(0) - jnp.broadcast_to(col[:, k : k + 1], (8, LANES))
                    dy = chan(1) - jnp.broadcast_to(col[:, 4 + k : 5 + k], (8, LANES))
                    dz = chan(2) - oz
                    d2 = dx * dx + dy * dy + dz * dz
                    w = jnp.maximum(1.0 - d2 * INV_RADIUS_SQ, 0.0)
                    for c in range(3):
                        term = w * chan(3 + c)
                        totals[c] = term if k == 0 else totals[c] + term
                for c in range(3):
                    acc[c, place, :] = totals[c]
            return 0

        lax.fori_loop(0, LANES // GROUP, some, 0)
        own = meta[0:1, span]
        mine = own_iota == own
        hot = jnp.where(mine, 1.0, 0.0)
        before = jnp.dot(hot.astype(jnp.bfloat16), tri[...], preferred_element_type=jnp.float32)
        rank = jnp.sum(jnp.where(mine, before + carry, 0.0), axis=0, keepdims=True)
        values = []
        for c in range(3):
            sums = lax.dot_general(
                ones, acc[c], NT, precision=HIGHEST, preferred_element_type=jnp.float32
            )
            rad = sums[0:1] * alb[c : c + 1, span]
            high = rad.astype(jnp.bfloat16).astype(jnp.float32)
            values += [high, rad - high]
        values += [meta[1:2, span].astype(jnp.float32), meta[2:3, span].astype(jnp.float32)]
        left = jnp.concatenate(
            [jnp.where(mine, v, 0.0).astype(jnp.bfloat16) for v in values], axis=0
        )
        right = jnp.where(cap_iota == rank, 1.0, 0.0).astype(jnp.bfloat16)
        packed[...] += lax.dot_general(left, right, NT, preferred_element_type=jnp.float32)
        return carry + jnp.sum(hot, axis=1, keepdims=True)

    lax.fori_loop(0, points // LANES, block, jnp.zeros((owners, 1), jnp.float32))
    pitch = out.shape[0] // owners

    def part(v, j):
        return packed[pl.ds(v * owners, owners), pl.ds(j * LANES, LANES)]

    for j in range(cap_rows):
        for c in range(3):
            out[pl.ds(c * cap_rows + j, owners, stride=pitch), :] = part(2 * c, j) + part(2 * c + 1, j)
        out[pl.ds(3 * cap_rows + j, owners, stride=pitch), :] = part(6, j)
        out[pl.ds(4 * cap_rows + j, owners, stride=pitch), :] = part(7, j)
    for r in range(5 * cap_rows, pitch):
        out[pl.ds(r, owners, stride=pitch), :] = jnp.zeros((owners, LANES), jnp.float32)


def pack_radiance(idx, pts, alb, meta, first, photons, halo, owners, cap_rows):
    cells = first.shape[0]
    rows = cells + halo.shape[1]
    pitch = -(-5 * cap_rows // 8) * 8
    vm = pl.BlockSpec(memory_space=pltpu.VMEM)
    hb = pl.BlockSpec(memory_space=pl.ANY)
    return pl.pallas_call(
        functools.partial(radiance_kernel, cells, rows, owners, cap_rows),
        out_shape=jax.ShapeDtypeStruct((owners * pitch, LANES), jnp.float32),
        in_specs=[pl.BlockSpec(memory_space=pltpu.SMEM), vm, vm, vm, hb, hb, hb],
        out_specs=vm,
        scratch_shapes=[
            pltpu.VMEM((6 * rows, LANES), jnp.float32),
            pltpu.VMEM((4 * 6 * GROUP, LANES), jnp.float32),
            pltpu.VMEM((LANES, pts.shape[0]), jnp.float32),
            pltpu.VMEM((3, LANES, LANES), jnp.float32),
            pltpu.VMEM((8 * owners, cap_rows * LANES), jnp.float32),
            pltpu.VMEM((LANES, LANES), jnp.bfloat16),
            pltpu.SemaphoreType.DMA((12,)),
        ],
        name="radiance",
    )(idx, pts, alb, meta, first, photons, halo)


def film_kernel(nx, ny, cap_rows, unroll, send, out, recv, send_sem, recv_sem, own_sem):
    count = nx * ny
    ix, iy = lax.axis_index("bx"), lax.axis_index("by")
    me = ix * ny + iy
    barrier = pltpu.get_barrier_semaphore()

    def greet(s, _):
        to = lax.rem(me + s, count)
        pl.semaphore_signal(
            barrier, inc=1, device_id=(to // ny, lax.rem(to, ny)), device_id_type=MESH
        )
        return 0

    lax.fori_loop(1, count, greet, 0)
    own = pltpu.make_async_copy(send.at[me], recv.at[me], own_sem)
    own.start()
    pl.semaphore_wait(barrier, count - 1)

    def copy_to(s):
        to = lax.rem(me + s, count)
        return pltpu.make_async_remote_copy(
            src_ref=send.at[to],
            dst_ref=recv.at[me],
            send_sem=send_sem.at[to],
            recv_sem=recv_sem.at[me],
            device_id=(to // ny, lax.rem(to, ny)),
            device_id_type=MESH,
        )

    def go(s, _):
        copy_to(s).start()
        return 0

    lax.fori_loop(1, count, go, 0)
    own.wait()

    def arrive(s, _):
        come = lax.rem(me + count - s, count)
        pltpu.make_async_remote_copy(
            src_ref=send.at[come],
            dst_ref=recv.at[come],
            send_sem=send_sem.at[come],
            recv_sem=recv_sem.at[come],
            device_id=(come // ny, lax.rem(come, ny)),
            device_id_type=MESH,
        ).wait_recv()
        return 0

    lax.fori_loop(1, count, arrive, 0)

    tiles = out.shape[1]
    halves = out.shape[2] // LANES
    high_rows = tiles * halves
    high_iota = lax.broadcasted_iota(jnp.int32, (high_rows, LANES), 0).astype(jnp.float32)
    low_iota = lax.broadcasted_iota(jnp.int32, (LANES, LANES), 0).astype(jnp.float32)

    def add(step, total):
        lefts, rights = [], []
        for u in range(unroll):
            blk = recv[step * unroll + u]
            for j in range(cap_rows):
                def row(v):
                    r = v * cap_rows + j
                    return blk[r : r + 1]
                here = high_iota == row(3)
                parts = []
                for c in range(3):
                    value = row(c)
                    top = value.astype(jnp.bfloat16).astype(jnp.float32)
                    parts += [jnp.where(here, top, 0.0), jnp.where(here, value - top, 0.0)]
                lefts.append(jnp.concatenate(parts, axis=0).astype(jnp.bfloat16))
                rights.append(jnp.where(low_iota == row(4), 1.0, 0.0).astype(jnp.bfloat16))
        left = jnp.concatenate(lefts, axis=1)
        right = jnp.concatenate(rights, axis=1)
        return total + lax.dot_general(left, right, NT, preferred_element_type=jnp.float32)

    total = lax.fori_loop(
        0, count // unroll, add, jnp.zeros((6 * high_rows, LANES), jnp.float32)
    )
    for c in range(3):
        for h in range(halves):
            at = 2 * c * high_rows + h * tiles
            out[c, :, h * LANES : (h + 1) * LANES] = (
                total[at : at + tiles] + total[at + high_rows : at + high_rows + tiles]
            )

    def sent(s, _):
        copy_to(s).wait_send()
        return 0

    lax.fori_loop(1, count, sent, 0)


def gather_film(send, nx, ny, cap_rows, tiles):
    count = nx * ny
    return pl.pallas_call(
        functools.partial(film_kernel, nx, ny, cap_rows, 4),
        out_shape=jax.ShapeDtypeStruct((3, tiles, TILE_PIX), jnp.float32),
        in_specs=[pl.BlockSpec(memory_space=pltpu.VMEM)],
        out_specs=pl.BlockSpec(memory_space=pltpu.VMEM),
        scratch_shapes=[
            pltpu.VMEM(send.shape, jnp.float32),
            pltpu.SemaphoreType.DMA((count,)),
            pltpu.SemaphoreType.DMA((count,)),
            pltpu.SemaphoreType.DMA,
        ],
        compiler_params=pltpu.CompilerParams(collective_id=1, has_side_effects=True),
        name="film",
    )(send)


def per_device(
    nx, ny, photon_data, block_counts, gather_offsets, gather_blocks, albedo, gather_pixels, tile_slot
):
    cx, cy, slots = photon_data.shape[1:]
    grid_x, grid_y = cx * nx, cy * ny
    points = gather_offsets.shape[1]
    owners = nx * ny
    tiles = tile_slot.shape[0]
    tiles_dev = tiles // owners
    cap_rows = -(-(3 * points // owners) // LANES)

    live = lax.broadcasted_iota(jnp.int32, (cx, cy, slots), 2) < block_counts[:, :, None]
    first = jnp.where(live, photon_data[0], FAR)

    def edge(x, y):
        a = first[x, y].reshape(1, -1, slots)
        b = photon_data[1:, x, y].reshape(5, -1, slots)
        return jnp.concatenate([a, b], axis=0)

    every = slice(None)
    tail, head = slice(cy - 8, cy), slice(0, 8)
    send = jnp.concatenate(
        [
            edge(cx - 1, every),
            edge(0, every),
            edge(every, cy - 1),
            edge(every, 0),
            edge(cx - 1, tail),
            edge(cx - 1, head),
            edge(0, tail),
            edge(0, head),
        ],
        axis=1,
    )
    halo = exchange_halo(send, nx, ny, cx, cy)

    first_x = lax.axis_index("bx") * cx
    first_y = lax.axis_index("by") * cy
    lx = (gather_blocks // grid_y - first_x + 1) % grid_x
    ly = (gather_blocks % grid_y - first_y + 1) % grid_y
    shift_x = (lx - lx[:1]).astype(jnp.float32)
    shift_y = (ly - ly[:1]).astype(jnp.float32)
    cells = cx * cy
    x_out = (lx == 0) | (lx == cx + 1)
    y_out = (ly == 0) | (ly == cy + 1)
    x_far = (lx == cx + 1).astype(jnp.int32)
    y_far = (ly == cy + 1).astype(jnp.int32)
    corner = 2 * cy + 2 * cx + 16 * x_far + 8 * y_far + 7 * (1 - y_far)
    index = jnp.where(
        x_out,
        jnp.where(y_out, cells + corner, cells + x_far * cy + ly - 1),
        jnp.where(y_out, cells + 2 * cy + y_far * cx + lx - 1, (lx - 1) * cy + ly - 1),
    )
    pts = jnp.concatenate(
        [
            gather_offsets[0:1] - shift_x,
            gather_offsets[1:2] - shift_y,
            gather_offsets[2:3],
            jnp.zeros((7, points), jnp.float32),
        ],
        axis=0,
    )
    tile = gather_pixels // TILE_PIX
    matched = tile[:, None] == jnp.arange(tiles, dtype=jnp.int32)[None, :]
    slot = jnp.sum(jnp.where(matched, tile_slot[None, :], 0), axis=1)
    within = gather_pixels % TILE_PIX
    meta = jnp.stack(
        [slot // tiles_dev, (within // LANES) * tiles_dev + slot % tiles_dev, within % LANES]
    )
    packed = pack_radiance(
        index.reshape(-1), pts, albedo, meta, first.reshape(cells, slots),
        photon_data.reshape(6, cells, slots), halo, owners, cap_rows,
    )
    return gather_film(packed.reshape(owners, -1, LANES), nx, ny, cap_rows, tiles_dev)


def solution(mesh):
    both = ("bx", "by")
    in_specs = (
        P(None, "bx", "by", None), P("bx", "by"), P(None, both), P(None, both),
        P(None, both), P(both), P(),
    )
    return jax.shard_map(
        functools.partial(per_device, mesh.shape["bx"], mesh.shape["by"]),
        mesh=mesh, in_specs=in_specs, out_specs=P(None, both, None), check_vma=False,
    )
```

time: 608 us -> 151 us (0.25)
  local copies, waits for them, and re-layouts: 243 us -> 9.84 us
  other arithmetic: 194 us -> 9.16 us
  waiting for transfers between devices: 145 us -> 0 us
  Pallas kernels: 0 us -> 131 us
  between operations: 13.5 us -> 0.18 us
  starting transfers between devices: 7.78 us -> 0 us
    gather x8 -> x0, local copies, waits for them, and re-layouts: 155 us -> none  [one_group(): jnp.take(table, idb.reshape(-1), axis=1).reshape(6, group, listed, slots)]
    reduce_scatter x1 -> x0, waiting for transfers between devices: 136 us -> none  [per_device(): lax.psum_scatter(partial_film, ('bx', 'by'), scatter_dimension=1, tiled=T...]
    pallas_call x0 -> x3, Pallas kernels: none -> 131 us  [the longest x1 96.3 us: pack_radiance(): pl.pallas_call(functools.partial(radiance_kernel, cells, rows, owners, ca...]
    select_n x17 -> x3, other arithmetic: 89.7 us -> 2.94 us  [the longest x2 2.87 us: per_device(): first = jnp.where(live, photon_data[0], FAR)]
    scatter-add x1 -> x0, other arithmetic: 35.5 us -> none  [per_device(): jnp.zeros((3, tiles * TILE_PIX), jnp.float32).at[:, target].add(radiance)]
    reduce_sum x16 -> x0, other arithmetic: 34.3 us -> none  [kernel_sum(): sums = jnp.sum(weight[None] * blocks[3:6], axis=(2, 3))]
    reshape x18 -> x0, local copies, waits for them, and re-layouts: 22.9 us -> none  [the longest x1 19.5 us: per_device(): partial_film = partial_film.reshape(3, tiles, TILE_PIX)]
    slice x20 -> x8, local copies, waits for them, and re-layouts: 24.2 us -> 4.33 us  [the longest x1 1.95 us: edge(): b = photon_data[1:, x, y].reshape(5, -1, slots)]
  transfers between devices with their start and end apart: 5 -> 0, of which waited for: 3 -> 0; matrix products, arithmetic and copies ran while one was open for 2% -> 0% of each run, Pallas kernels for 0% -> 0%
where the time goes in v1:
time: 151 us; the launch traced here: 150 us
  Pallas kernels  131 us (87%)
  local copies, waits for them, and re-layouts  9.84 us (7%)
  other arithmetic  9.16 us (6%)
    pallas_call x1, Pallas kernels, pack_radiance(): pl.pallas_call(functools.partial(radiance_kernel, cells, rows, owners, ca...  96.3 us
    pallas_call x1, Pallas kernels, gather_film(): pl.pallas_call(functools.partial(film_kernel, nx, ny, cap_rows, 4), out_s...  17.4 us
    pallas_call x1, Pallas kernels, exchange_halo(): pl.pallas_call(functools.partial(halo_kernel, nx, ny, cx, cy), out_shape=...  17.4 us
    unnamed x5, local copies, waits for them, and re-layouts  3.63 us

profile of v1, /device:TPU:0, one launch (start us, length us, event | category | flops | bytes accessed | tf_op | source)
XLA Modules:
  0.0 150.3 jit_solution(770733120702854787)
XLA Ops:
  0.0 0.1 pad.22.clone
  0.1 0.7 add_select_fusion.8
  0.8 2.0 %select_reduce_fusion = s32[4096]{0:T(1024)S(1)} fusion(s32[256]{0:T(256)} %param.13, s32[4096]{0:T(1024)S(1)} %add_select_fusion.8), kind=kLoop, calls=%fused_computation | loop fusion | flops 3141632 | bytes 33792 | tf_op jit(solution)/shard_map/reduce_sum | solution.py:370
  2.8 0.1 and_select_fusion
  2.9 0.8 copy.27
  3.7 0.1 lt.49
  3.7 0.8 fusion.9
  4.5 0.7 pad_add_fusion.meta
  5.2 1.0 fusion.19
  6.2 0.8 slice_bitcast_fusion.2
  7.0 0.9 slice_bitcast_fusion
  7.9 1.2 select_bitcast_fusion
  9.1 0.6 copy.45
  9.8 0.1 convert_subtract_fusion
  9.8 0.8 maximum_maximum_fusion.pts
  10.6 2.0 %fusion.15 = (f32[5,64,1,128]{3,2,1,0:T(1,128)S(1)}, f32[5,64,1,128]{3,2,1,0:T(1,128)S(1)}) fusion(f32[6,64,32,128]{3,2,1,0:T(8,128)} %param.7), kind=kLoop, calls=%fused_computation.74 | loop fusion | bytes 655360 | tf_op jit(solution)/shard_map/slice | solution.py:322
  12.6 1.6 %bitcast_select_fusion = f32[64,32,128]{2,1,0:T(8,128)S(1)} fusion(s32[64,32]{1,0:T(8,128)S(1)} %copy.27, f32[6,64,32,128]{3,2,1,0:T(8,128)} %param.7), kind=kLoop, calls=%fused_computation.2 | loop fusion | flops 524288 | bytes 2105344 | tf_op jit(solution)/shard_map/jit(_where)/select_n | solution.py:318
  14.3 0.0 copy-start
  14.4 0.8 copy-done
  15.2 17.4 %halo.1 = f32[6,224,128]{2,1,0:T(8,128)} custom-call(f32[6,224,128]{2,1,0:T(8,128)} %copy-done), custom_call_target="tpu_custom_call" | custom-call | tf_op jit(solution)/shard_map/halo/pallas_call | solution.py:58
  32.6 1.3 slice.71
  33.9 1.3 bitcast_select_fusion.1.first
  35.2 96.3 %radiance.1 = f32[512,128]{1,0:T(8,128)} custom-call(s32[16384]{0:T(1024)} %bitcast.52, f32[16,4096]{1,0:T(8,128)} %maximum_maximum_fusion.pts, f32[3,4096]{1,0:T(4,128)} %alb.1, s32[3,4096]{1,0:T(4,128)} %pad_add_fusion.meta, f32[2048,128]{1,0:T(8,128)} %bitcast_select_fusion.1.first, f32[6,2048,128]{2,1,0:T(8,128)} %bitcast.48, f32[6,224,128]{2,1,0:T(8,128)} %halo.1), custom_call_target="tpu_custom_call" | custom-call | tf_op jit(solution)/shard_map/radiance/pallas_call | solution.py:177
  131.5 17.4 %film.1 = f32[3,8,256]{2,1,0:T(8,128)} custom-call(f32[32,16,128]{2,1,0:T(8,128)} %bitcast.49), custom_call_target="tpu_custom_call" | custom-call | tf_op jit(solution)/shard_map/film/pallas_call | solution.py:290
  149.0 1.3 copy.54
  (14 shorter events, 0.2 us)
Async XLA Ops:
  14.3 0.9 copy-start

commit v2 on v1

--- a/solution.py
+++ b/solution.py
@@ -12,9 +12,8 @@
 FAR = 1.0e4
 LANES = 128
 MESH = pl.DeviceIdType.MESH
-HIGHEST = lax.Precision.HIGHEST
 NT = (((1,), (1,)), ((), ()))
-GROUP = 32
+PITCH = LANES + 1
 
 
 def halo_kernel(nx, ny, cx, cy, send, recv, send_sem, recv_sem):
@@ -69,21 +68,17 @@
 def radiance_kernel(
     cells, rows, owners, cap_rows,
     idx, pts, alb, meta, first, rest, halo, out,
-    table, stage, cols, acc, packed, tri, sems,
+    table, stage, wide, acc, packed, tri, spread, sems,
 ):
     listed = 4
     points = pts.shape[1]
-    fills = [
-        pltpu.make_async_copy(first, table.at[pl.ds(0, cells)], sems.at[0]),
-    ]
+    fills = [pltpu.make_async_copy(first, table.at[pl.ds(0, cells), 0], sems.at[0])]
     for c in range(1, 6):
-        fills.append(
-            pltpu.make_async_copy(rest.at[c], table.at[pl.ds(c * rows, cells)], sems.at[c])
-        )
+        fills.append(pltpu.make_async_copy(rest.at[c], table.at[pl.ds(0, cells), c], sems.at[c]))
     for c in range(6):
         fills.append(
             pltpu.make_async_copy(
-                halo.at[c], table.at[pl.ds(c * rows + cells, rows - cells)], sems.at[6 + c]
+                halo.at[c], table.at[pl.ds(cells, rows - cells), c], sems.at[6 + c]
             )
         )
     for fill in fills:
@@ -91,47 +86,55 @@
     a = lax.broadcasted_iota(jnp.int32, (LANES, LANES), 0)
     b = lax.broadcasted_iota(jnp.int32, (LANES, LANES), 1)
     tri[...] = jnp.where(a < b, 1.0, 0.0).astype(jnp.bfloat16)
+    a = lax.broadcasted_iota(jnp.int32, spread.shape, 0)
+    b = lax.broadcasted_iota(jnp.int32, spread.shape, 1)
+    spread[...] = jnp.where(a % 16 == b // LANES, 1.0, 0.0).astype(jnp.bfloat16)
     packed[...] = jnp.zeros_like(packed)
+    own_iota = lax.broadcasted_iota(jnp.int32, (owners, LANES), 0)
+    cap_iota = lax.broadcasted_iota(jnp.int32, (cap_rows * LANES, LANES), 0).astype(jnp.float32)
     for fill in fills:
         fill.wait()
-    ones = jnp.ones((8, LANES), jnp.float32)
-    own_iota = lax.broadcasted_iota(jnp.int32, (owners, LANES), 0)
-    cap_iota = lax.broadcasted_iota(jnp.int32, (cap_rows * LANES, LANES), 0).astype(jnp.float32)
 
     def block(blk, carry):
         base = pl.multiple_of(blk * LANES, LANES)
         span = pl.ds(base, LANES)
-        cols[...] = pts[:, span].T
-
-        def some(sub, _):
-            start = sub * GROUP
-            for p in range(GROUP):
-                for k in range(listed):
-                    row = idx[k * points + base + start + p]
-                    stage[pl.ds(k * 6 * GROUP + p, 6, stride=GROUP), :] = table[
-                        pl.ds(row, 6, stride=rows), :
-                    ]
-            for q in range(GROUP // 8):
-                place = pl.ds(pl.multiple_of(start + q * 8, 8), 8)
-                col = cols[place, :]
-                oz = jnp.broadcast_to(col[:, 8:9], (8, LANES))
-                totals = [None] * 3
-                for k in range(listed):
-                    def chan(c):
-                        return stage[pl.ds((k * 6 + c) * GROUP + q * 8, 8), :]
-                    dx = chan(0) - jnp.broadcast_to(col[:, k : k + 1], (8, LANES))
-                    dy = chan(1) - jnp.broadcast_to(col[:, 4 + k : 5 + k], (8, LANES))
-                    dz = chan(2) - oz
-                    d2 = dx * dx + dy * dy + dz * dz
-                    w = jnp.maximum(1.0 - d2 * INV_RADIUS_SQ, 0.0)
-                    for c in range(3):
-                        term = w * chan(3 + c)
-                        totals[c] = term if k == 0 else totals[c] + term
+        value = pts[:, span]
+        parts = []
+        for _ in range(3):
+            high = value.astype(jnp.bfloat16)
+            parts.append(high)
+            value = value - high.astype(jnp.float32)
+        wide[...] = lax.dot_general(
+            jnp.concatenate(parts, axis=0), spread[...], (((0,), (0,)), ((), ())),
+            preferred_element_type=jnp.float32,
+        )
+        for p in range(LANES):
+            for k in range(listed):
+                stage[pl.ds(k * 8 * PITCH + p, 8, stride=PITCH), :] = table[
+                    idx[k * points + base + p]
+                ]
+        for q in range(LANES // 8):
+            place = slice(q * 8, q * 8 + 8)
+
+            def column(n):
+                return wide[place, n * LANES : (n + 1) * LANES]
+
+            oz = column(8)
+            totals = [None] * 3
+            for k in range(listed):
+                def chan(c):
+                    return stage[pl.ds((k * 8 + c) * PITCH + q * 8, 8), :]
+
+                dx = chan(0) - column(k)
+                dy = chan(1) - column(4 + k)
+                dz = chan(2) - oz
+                d2 = dx * dx + dy * dy + dz * dz
+                w = jnp.maximum(1.0 - d2 * INV_RADIUS_SQ, 0.0)
                 for c in range(3):
-                    acc[c, place, :] = totals[c]
-            return 0
-
-        lax.fori_loop(0, LANES // GROUP, some, 0)
+                    term = w * chan(3 + c)
+                    totals[c] = term if k == 0 else totals[c] + term
+            for c in range(3):
+                acc[c, place, :] = totals[c]
         own = meta[0:1, span]
         mine = own_iota == own
         hot = jnp.where(mine, 1.0, 0.0)
@@ -139,10 +142,7 @@
         rank = jnp.sum(jnp.where(mine, before + carry, 0.0), axis=0, keepdims=True)
         values = []
         for c in range(3):
-            sums = lax.dot_general(
-                ones, acc[c], NT, precision=HIGHEST, preferred_element_type=jnp.float32
-            )
-            rad = sums[0:1] * alb[c : c + 1, span]
+            rad = jnp.sum(acc[c].T, axis=0, keepdims=True) * alb[c : c + 1, span]
             high = rad.astype(jnp.bfloat16).astype(jnp.float32)
             values += [high, rad - high]
         values += [meta[1:2, span].astype(jnp.float32), meta[2:3, span].astype(jnp.float32)]
@@ -180,12 +180,13 @@
         in_specs=[pl.BlockSpec(memory_space=pltpu.SMEM), vm, vm, vm, hb, hb, hb],
         out_specs=vm,
         scratch_shapes=[
-            pltpu.VMEM((6 * rows, LANES), jnp.float32),
-            pltpu.VMEM((4 * 6 * GROUP, LANES), jnp.float32),
-            pltpu.VMEM((LANES, pts.shape[0]), jnp.float32),
+            pltpu.VMEM((rows, 8, LANES), jnp.float32),
+            pltpu.VMEM((4 * 8 * PITCH + 8, LANES), jnp.float32),
+            pltpu.VMEM((LANES, 9 * LANES), jnp.float32),
             pltpu.VMEM((3, LANES, LANES), jnp.float32),
             pltpu.VMEM((8 * owners, cap_rows * LANES), jnp.float32),
             pltpu.VMEM((LANES, LANES), jnp.bfloat16),
+            pltpu.VMEM((48, 9 * LANES), jnp.bfloat16),
             pltpu.SemaphoreType.DMA((12,)),
         ],
         name="radiance",

time: 151 us -> 91.7 us (0.61)
  Pallas kernels: 131 us -> 71.8 us
    pallas_call x1, Pallas kernels: 96.3 us -> 36.9 us  [pack_radiance(): pl.pallas_call(functools.partial(radiance_kernel, cells, rows, owners, ca...]
where the time goes in v2:
time: 91.7 us; the launch traced here: 90.9 us
  Pallas kernels  71.8 us (78%)
  local copies, waits for them, and re-layouts  9.84 us (11%)
  other arithmetic  9.16 us (10%)
    pallas_call x1, Pallas kernels, pack_radiance(): pl.pallas_call(functools.partial(radiance_kernel, cells, rows, owners, ca...  36.9 us
    pallas_call x1, Pallas kernels, gather_film(): pl.pallas_call(functools.partial(film_kernel, nx, ny, cap_rows, 4), out_s...  17.4 us
    pallas_call x1, Pallas kernels, exchange_halo(): pl.pallas_call(functools.partial(halo_kernel, nx, ny, cx, cy), out_shape=...  17.4 us
    unnamed x5, local copies, waits for them, and re-layouts  3.63 us
    select_n x2, other arithmetic, per_device(): first = jnp.where(live, photon_data[0], FAR)  2.87 us
    reduce_sum x1, other arithmetic, per_device(): slot = jnp.sum(jnp.where(matched, tile_slot[None, :], 0), axis=1)  1.96 us
    slice x1, local copies, waits for them, and re-layouts, edge(): b = photon_data[1:, x, y].reshape(5, -1, slots)  1.95 us

profile of v2, /device:TPU:0, one launch (start us, length us, event | category | flops | bytes accessed | tf_op | source)
XLA Modules:
  0.0 90.9 jit_solution(4279755307340612999)
XLA Ops:
  0.0 0.1 pad.22.clone
  0.1 0.7 add_select_fusion.8
  0.8 2.0 %select_reduce_fusion = s32[4096]{0:T(1024)S(1)} fusion(s32[256]{0:T(256)} %param.13, s32[4096]{0:T(1024)S(1)} %add_select_fusion.8), kind=kLoop, calls=%fused_computation | loop fusion | flops 3141632 | bytes 33792 | tf_op jit(solution)/shard_map/reduce_sum | solution.py:371
  2.8 0.1 and_select_fusion
  2.9 0.8 copy.27
  3.7 0.1 lt.49
  3.7 0.8 fusion.9
  4.5 0.7 pad_add_fusion.meta
  5.2 1.0 %fusion.19 = (f32[1,4096]{1,0:T(1,128)S(1)}, f32[1,4096]{1,0:T(1,128)S(1)}, f32[1,4096]{1,0:T(1,128)S(1)}) fusion(f32[3,4096]{1,0:T(4,128)} %param.9), kind=kLoop, calls=%fused_computation.78 | loop fusion | bytes 98304 | tf_op jit(solution)/shard_map/slice | solution.py:362
  6.2 0.8 slice_bitcast_fusion.2
  7.0 0.9 %slice_bitcast_fusion = (f32[5,32,128]{2,1,0:T(8,128)S(1)}, f32[5,32,128]{2,1,0:T(8,128)S(1)}) fusion(f32[6,64,32,128]{3,2,1,0:T(8,128)} %param.7), kind=kLoop, calls=%fused_computation.22 | loop fusion | bytes 327680 | tf_op jit(solution)/shard_map/squeeze | solution.py:323
  7.9 1.2 %select_bitcast_fusion = (s32[1,32,4,128]{3,2,1,0:T(4,128)S(1)}, s32[4,4096]{1,0:T(4,128)S(1)}, s32[4,4096]{1,0:T(4,128)S(1)}) fusion(s32[]{:T(128)S(6)} %mul.38, s32[4,4096]{1,0:T(4,128)} %param.10, s32[]{:T(128)S(6)} %mul.39), kind=kLoop, calls=%fused_computation.33 | loop fusion | flops 1228800 | bytes 262152
  9.1 0.6 copy.45
  9.8 0.1 convert_subtract_fusion
  9.8 0.8 maximum_maximum_fusion.pts
  10.6 2.0 %fusion.15 = (f32[5,64,1,128]{3,2,1,0:T(1,128)S(1)}, f32[5,64,1,128]{3,2,1,0:T(1,128)S(1)}) fusion(f32[6,64,32,128]{3,2,1,0:T(8,128)} %param.7), kind=kLoop, calls=%fused_computation.74 | loop fusion | bytes 655360 | tf_op jit(solution)/shard_map/slice | solution.py:323
  12.6 1.6 %bitcast_select_fusion = f32[64,32,128]{2,1,0:T(8,128)S(1)} fusion(s32[64,32]{1,0:T(8,128)S(1)} %copy.27, f32[6,64,32,128]{3,2,1,0:T(8,128)} %param.7), kind=kLoop, calls=%fused_computation.2 | loop fusion | flops 524288 | bytes 2105344 | tf_op jit(solution)/shard_map/jit(_where)/select_n | solution.py:319
  14.3 0.0 copy-start
  14.4 0.8 copy-done
  15.2 17.4 %halo.1 = f32[6,224,128]{2,1,0:T(8,128)} custom-call(f32[6,224,128]{2,1,0:T(8,128)} %copy-done), custom_call_target="tpu_custom_call" | custom-call | tf_op jit(solution)/shard_map/halo/pallas_call | solution.py:57
  32.6 1.3 %slice.71 = f32[1,64,32,128]{3,2,1,0:T(8,128)S(1)} slice(f32[6,64,32,128]{3,2,1,0:T(8,128)} %param.7), slice={[0:1], [0:64], [0:32], [0:128]} | slice | bytes 2097152 | tf_op jit(solution)/shard_map/slice | solution.py:319
  33.9 1.3 %bitcast_select_fusion.1.first = f32[2048,128]{1,0:T(8,128)} fusion(f32[1,64,32,128]{3,2,1,0:T(8,128)S(1)} %slice.71, s32[2048]{0:T(1024)S(1)} %lt.49), kind=kLoop, calls=%fused_computation.3 | loop fusion | flops 524288 | bytes 2105344 | tf_op jit(solution)/shard_map/jit(_where)/select_n | solution.py:319
  35.2 36.9 %radiance.1 = f32[512,128]{1,0:T(8,128)} custom-call(s32[16384]{0:T(1024)} %bitcast.52, f32[16,4096]{1,0:T(8,128)} %maximum_maximum_fusion.pts, f32[3,4096]{1,0:T(4,128)} %alb.1, s32[3,4096]{1,0:T(4,128)} %pad_add_fusion.meta, f32[2048,128]{1,0:T(8,128)} %bitcast_select_fusion.1.first, f32[6,2048,128]{2,1,0:T(8,128)} %bitcast.48, f32[6,224,128]{2,1,0:T(8,128)} %halo.1), custom_call_target="tpu_custom_call" | custom-call | tf_op jit(solution)/shard_map/radiance/pallas_call | solution.py:177
  72.1 17.4 %film.1 = f32[3,8,256]{2,1,0:T(8,128)} custom-call(f32[32,16,128]{2,1,0:T(8,128)} %bitcast.49), custom_call_target="tpu_custom_call" | custom-call | tf_op jit(solution)/shard_map/film/pallas_call | solution.py:291
  89.6 1.3 %copy.54 = f32[3,8,256]{2,1,0:T(8,128)} copy(f32[3,8,256]{2,1,0:T(8,128)} %film.1) | data formatting | bytes 49152
  (14 shorter events, 0.2 us)
Async XLA Ops:
  14.3 0.9 copy-start

commit v3 on v2

--- a/solution.py
+++ b/solution.py
@@ -16,7 +16,7 @@
 PITCH = LANES + 1
 
 
-def halo_kernel(nx, ny, cx, cy, send, recv, send_sem, recv_sem):
+def halo_kernel(nx, ny, cx, cy, first, photons, recv, send, send_sem, recv_sem, edge_sem):
     ix, iy = lax.axis_index("bx"), lax.axis_index("by")
     right, left = lax.rem(ix + 1, nx), lax.rem(ix + nx - 1, nx)
     up, down = lax.rem(iy + 1, ny), lax.rem(iy + ny - 1, ny)
@@ -30,6 +30,26 @@
         (left, up, 2 * cy + 2 * cx + 16, 8),
         (left, down, 2 * cy + 2 * cx + 24, 8),
     ]
+    every, tail, head = pl.ds(0, cy), pl.ds(cy - 8, 8), pl.ds(0, 8)
+    wide = pl.ds(0, cx)
+    cuts = [
+        (cx - 1, every), (0, every), (wide, cy - 1), (wide, 0),
+        (cx - 1, tail), (cx - 1, head), (0, tail), (0, head),
+    ]
+    edges = []
+    for n, (x, y) in enumerate(cuts):
+        part = pl.ds(peers[n][2], peers[n][3])
+        edges.append(
+            pltpu.make_async_copy(
+                photons.at[pl.ds(1, 5), x, y], send.at[pl.ds(1, 5), part], edge_sem.at[2 * n]
+            )
+        )
+        edges.append(
+            pltpu.make_async_copy(first.at[x, y], send.at[0, part], edge_sem.at[2 * n + 1])
+        )
+    for n in (2, 3, 0, 1, 4, 5, 6, 7):
+        edges[2 * n].start()
+        edges[2 * n + 1].start()
     barrier = pltpu.get_barrier_semaphore()
     for px, py, _, _ in peers:
         pl.semaphore_signal(barrier, inc=1, device_id=(px, py), device_id_type=MESH)
@@ -48,21 +68,29 @@
             )
         )
     for n in (2, 3, 0, 1, 4, 5, 6, 7):
+        edges[2 * n].wait()
+        edges[2 * n + 1].wait()
         copies[n].start()
     for copy in copies:
         copy.wait()
 
 
-def exchange_halo(send, nx, ny, cx, cy):
+def exchange_halo(first, photons, nx, ny, cx, cy):
+    shape = (6, 2 * cy + 2 * cx + 32, photons.shape[3])
     return pl.pallas_call(
         functools.partial(halo_kernel, nx, ny, cx, cy),
-        out_shape=jax.ShapeDtypeStruct(send.shape, jnp.float32),
-        in_specs=[pl.BlockSpec(memory_space=pl.ANY)],
+        out_shape=jax.ShapeDtypeStruct(shape, jnp.float32),
+        in_specs=[pl.BlockSpec(memory_space=pl.ANY)] * 2,
         out_specs=pl.BlockSpec(memory_space=pl.ANY),
-        scratch_shapes=[pltpu.SemaphoreType.DMA((8,)), pltpu.SemaphoreType.DMA((8,))],
+        scratch_shapes=[
+            pltpu.VMEM(shape, jnp.float32),
+            pltpu.SemaphoreType.DMA((8,)),
+            pltpu.SemaphoreType.DMA((8,)),
+            pltpu.SemaphoreType.DMA((16,)),
+        ],
         compiler_params=pltpu.CompilerParams(collective_id=0, has_side_effects=True),
         name="halo",
-    )(send)
+    )(first, photons)
 
 
 def radiance_kernel(
@@ -229,19 +257,21 @@
     lax.fori_loop(1, count, go, 0)
     own.wait()
 
-    def arrive(s, _):
+    def arrive(s):
         come = lax.rem(me + count - s, count)
-        pltpu.make_async_remote_copy(
-            src_ref=send.at[come],
-            dst_ref=recv.at[come],
-            send_sem=send_sem.at[come],
-            recv_sem=recv_sem.at[come],
-            device_id=(come // ny, lax.rem(come, ny)),
-            device_id_type=MESH,
-        ).wait_recv()
-        return 0
-
-    lax.fori_loop(1, count, arrive, 0)
+
+        @pl.when(s > 0)
+        def _():
+            pltpu.make_async_remote_copy(
+                src_ref=send.at[come],
+                dst_ref=recv.at[come],
+                send_sem=send_sem.at[come],
+                recv_sem=recv_sem.at[come],
+                device_id=(come // ny, lax.rem(come, ny)),
+                device_id_type=MESH,
+            ).wait_recv()
+
+        return come
 
     tiles = out.shape[1]
     halves = out.shape[2] // LANES
@@ -251,8 +281,9 @@
 
     def add(step, total):
         lefts, rights = [], []
-        for u in range(unroll):
-            blk = recv[step * unroll + u]
+        sources = [arrive(step * unroll + u) for u in range(unroll)]
+        for come in sources:
+            blk = recv[come]
             for j in range(cap_rows):
                 def row(v):
                     r = v * cap_rows + j
@@ -318,27 +349,8 @@
     live = lax.broadcasted_iota(jnp.int32, (cx, cy, slots), 2) < block_counts[:, :, None]
     first = jnp.where(live, photon_data[0], FAR)
 
-    def edge(x, y):
-        a = first[x, y].reshape(1, -1, slots)
-        b = photon_data[1:, x, y].reshape(5, -1, slots)
-        return jnp.concatenate([a, b], axis=0)
-
-    every = slice(None)
-    tail, head = slice(cy - 8, cy), slice(0, 8)
-    send = jnp.concatenate(
-        [
-            edge(cx - 1, every),
-            edge(0, every),
-            edge(every, cy - 1),
-            edge(every, 0),
-            edge(cx - 1, tail),
-            edge(cx - 1, head),
-            edge(0, tail),
-            edge(0, head),
-        ],
-        axis=1,
-    )
-    halo = exchange_halo(send, nx, ny, cx, cy)
+    first = lax.optimization_barrier(first)
+    halo = exchange_halo(first, photon_data, nx, ny, cx, cy)
 
     first_x = lax.axis_index("bx") * cx
     first_y = lax.axis_index("by") * cy

time: 91.7 us -> 83.7 us (0.913)
  local copies, waits for them, and re-layouts: 9.84 us -> 3.87 us
  Pallas kernels: 71.8 us -> 70.3 us
    slice x5 -> x0, local copies, waits for them, and re-layouts: 3.31 us -> none  [the longest x1 1.95 us: edge(): b = photon_data[1:, x, y].reshape(5, -1, slots)]
    squeeze x2 -> x0, local copies, waits for them, and re-layouts: 1.73 us -> none  [edge(): b = photon_data[1:, x, y].reshape(5, -1, slots)]
    pallas_call x1, Pallas kernels: 17.4 us -> 16.1 us  [gather_film(): pl.pallas_call(functools.partial(film_kernel, nx, ny, cap_rows, 4), out_s...]
    unnamed x5 -> x3, local copies, waits for them, and re-layouts: 3.63 us -> 2.77 us
    select_n x2 -> x1, other arithmetic: 2.87 us -> 2.54 us  [per_device(): first = jnp.where(live, photon_data[0], FAR)]
where the time goes in v3:
time: 83.7 us; the launch traced here: 83.1 us
  Pallas kernels  70.3 us (84%)
  other arithmetic  8.78 us (10%)
  local copies, waits for them, and re-layouts  3.87 us (5%)
    pallas_call x1, Pallas kernels, pack_radiance(): pl.pallas_call(functools.partial(radiance_kernel, cells, rows, owners, ca...  36.9 us
    pallas_call x1, Pallas kernels, exchange_halo(): pl.pallas_call(functools.partial(halo_kernel, nx, ny, cx, cy), out_shape=...  17.4 us
    pallas_call x1, Pallas kernels, gather_film(): pl.pallas_call(functools.partial(film_kernel, nx, ny, cap_rows, 4), out_s...  16.1 us
    unnamed x3, local copies, waits for them, and re-layouts  2.77 us
    select_n x1, other arithmetic, per_device(): first = jnp.where(live, photon_data[0], FAR)  2.54 us
    reduce_sum x1, other arithmetic, per_device(): slot = jnp.sum(jnp.where(matched, tile_slot[None, :], 0), axis=1)  1.96 us

profile of v3, /device:TPU:0, one launch (start us, length us, event | category | flops | bytes accessed | tf_op | source)
XLA Modules:
  0.0 83.1 jit_solution(13372362493702605054)
XLA Ops:
  0.0 0.1 pad.6.clone
  0.1 0.7 add_select_fusion.8
  0.8 2.0 %select_reduce_fusion = s32[4096]{0:T(1024)S(1)} fusion(s32[256]{0:T(256)} %param.13, s32[4096]{0:T(1024)S(1)} %add_select_fusion.8), kind=kLoop, calls=%fused_computation | loop fusion | flops 3141632 | bytes 33792 | tf_op jit(solution)/shard_map/reduce_sum | solution.py:383
  2.8 0.1 and_select_fusion
  2.9 0.8 copy.9
  3.7 0.8 fusion.9
  4.4 0.7 pad_add_fusion.meta
  5.1 1.0 %fusion.15 = (f32[1,4096]{1,0:T(1,128)S(1)}, f32[1,4096]{1,0:T(1,128)S(1)}, f32[1,4096]{1,0:T(1,128)S(1)}) fusion(f32[3,4096]{1,0:T(4,128)} %param.9), kind=kLoop, calls=%fused_computation.58 | loop fusion | bytes 98304 | tf_op jit(solution)/shard_map/slice | solution.py:374
  6.1 1.2 %select_bitcast_fusion = (s32[1,32,4,128]{3,2,1,0:T(4,128)S(1)}, s32[4,4096]{1,0:T(4,128)S(1)}, s32[4,4096]{1,0:T(4,128)S(1)}) fusion(s32[]{:T(128)S(6)} %mul.38, s32[4,4096]{1,0:T(4,128)} %param.10, s32[]{:T(128)S(6)} %mul.39), kind=kLoop, calls=%fused_computation.25 | loop fusion | flops 1228800 | bytes 262152
  7.3 0.6 copy.10
  8.0 0.1 convert_subtract_fusion
  8.0 0.8 maximum_maximum_fusion.pts
  8.8 2.5 %bitcast_select_fusion.first = f32[64,32,128]{2,1,0:T(8,128)} fusion(f32[6,64,32,128]{3,2,1,0:T(8,128)} %photons.1, s32[64,32]{1,0:T(8,128)S(1)} %copy.9), kind=kLoop, calls=%fused_computation.2 | loop fusion | flops 524288 | bytes 2105344 | tf_op jit(solution)/shard_map/jit(_where)/select_n | solution.py:350
  11.4 17.4 %halo.1 = f32[6,224,128]{2,1,0:T(8,128)} custom-call(f32[64,32,128]{2,1,0:T(8,128)} %bitcast_select_fusion.first, f32[6,64,32,128]{3,2,1,0:T(8,128)} %photons.1), custom_call_target="tpu_custom_call" | custom-call | tf_op jit(solution)/shard_map/halo/pallas_call | solution.py:80
  28.7 36.9 %radiance.1 = f32[512,128]{1,0:T(8,128)} custom-call(s32[16384]{0:T(1024)} %bitcast.18, f32[16,4096]{1,0:T(8,128)} %maximum_maximum_fusion.pts, f32[3,4096]{1,0:T(4,128)} %alb.1, s32[3,4096]{1,0:T(4,128)} %pad_add_fusion.meta, f32[2048,128]{1,0:T(8,128)} %bitcast.16, f32[6,2048,128]{2,1,0:T(8,128)} %bitcast.15, f32[6,224,128]{2,1,0:T(8,128)} %halo.1), custom_call_target="tpu_custom_call" | custom-call | tf_op jit(solution)/shard_map/radiance/pallas_call | solution.py:205
  65.6 16.1 %film.1 = f32[3,8,256]{2,1,0:T(8,128)} custom-call(f32[32,16,128]{2,1,0:T(8,128)} %bitcast.17), custom_call_target="tpu_custom_call" | custom-call | tf_op jit(solution)/shard_map/film/pallas_call | solution.py:322
  81.7 1.3 %copy.12 = f32[3,8,256]{2,1,0:T(8,128)} copy(f32[3,8,256]{2,1,0:T(8,128)} %film.1) | data formatting | bytes 49152
  (3 shorter events, 0.0 us)
